TPU v7x, 32 devices: a whole 2x2x4 slice. The times are simulated.
32 devices in a mesh: task: 4 (over y, x), tp: 8 (over z, core).
Axes of the slice: x: 2, y: 2, z: 4, core: 2. Of those that a mesh axis runs over, the one named last changes fastest.
Arguments:
- observations: bfloat16 [128, 16, 4096], P('task', None, 'tp'), may hold values from -6 to 6
- gain: float32 [4096], P('tp'), may hold values from 0.5 to 1.5
- w_in: bfloat16 [4096, 4096], P(None, 'tp'), may hold values from -0.09375 to 0.09375
- w_mix: bfloat16 [4096, 4096], P('tp'), may hold values from -0.09375 to 0.09375
- w_out: bfloat16 [4096, 4096], P(None, 'tp'), may hold values from -0.09375 to 0.09375
- w_head: bfloat16 [4096, 75], P('tp'), may hold values from -0.09375 to 0.09375
- head_bias: float32 [75], replicated, may hold values from -4 to 4
- pop_mean: float32 [57], replicated, may hold values from -8 to 8
- pop_scale: float32 [57], replicated, may hold values from 0.5 to 4
- task_indices: int32 [128], P('task'), may hold values from 0 to 56
- actions: int32 [128, 15], P('task'), may hold values from 0 to 17
- rewards: float32 [128, 15], P('task'), may hold values from -18 to 27
- episode_ends: int32 [128, 15], P('task'), may hold values 0 or 1
- behaviour_log_prob: float32 [128, 15], P('task'), may hold values from -4.5 to -1.5
Outputs:
- grad_w_in: float32 [4096, 4096], P(None, 'tp')
- grad_w_mix: float32 [4096, 4096], P('tp')
- grad_w_out: float32 [4096, 4096], P(None, 'tp')
- grad_gain: float32 [4096], P('tp')
- grad_head: float32 [4096, 75], P('tp')
- grad_head_bias: float32 [75], replicated
- new_head: bfloat16 [4096, 75], P('tp')
- new_bias: float32 [75], replicated
- updated_return_mean: float32 [57], replicated
- updated_return_scale: float32 [57], replicated
All inputs are finite; a program needn't handle non-finite values. No bound on the sum of `episode_ends` on one device may be relied on, other than what follows from the above.
Results may differ from a plain program's by a relative error of at most 0.03.
Values may be sent and summed in bfloat16 or wider, within the bound.
No kernel may reach another device: no remote copies, remote signals or barrier semaphores. Data moves between devices by JAX's collectives and lax.ppermute only.
A program may use at most 128 MiB of HBM per device.

v0:
```python
import jax
import jax.numpy as jnp
from jax import lax
from jax.sharding import PartitionSpec as P

ACTIONS = 18
TASKS = 57
DISCOUNT = 0.99
BASELINE_COST = 0.5
ENTROPY_COST = 0.01
POPART_PRIOR = 64.0
NORM_EPS = 1e-06


def silu_slope(before):
    sigmoid = jax.nn.sigmoid(before)
    return sigmoid * (1.0 + before * (1.0 - sigmoid))


def discounted_sums(values, factors):

    def advance(running, column):
        latest = column[0] + column[1] * running
        return (latest, latest)

    opening = jnp.zeros((values.shape[0],), jnp.float32)
    ending, stacked = lax.scan(advance, opening, (values.T, factors.T), reverse=True)
    return stacked.T


def task_onehot(task_indices):
    return (task_indices[:, None] == jnp.arange(TASKS, dtype=jnp.int32)[None, :]).astype(
        jnp.float32
    )


def popart_partials(task_indices, rewards, discount_factors):
    returns = discounted_sums(rewards, discount_factors)
    task_table = task_onehot(task_indices)
    counts = jnp.sum(task_table, axis=0) * rewards.shape[1]
    totals = jnp.dot(task_table.T, jnp.sum(returns, axis=1), precision=lax.Precision.HIGHEST)
    squares = jnp.dot(
        task_table.T, jnp.sum(returns * returns, axis=1), precision=lax.Precision.HIGHEST
    )
    return (counts, totals, squares)


def popart_update(counts, totals, squares, pop_mean, pop_scale):
    mixing = counts / (counts + POPART_PRIOR)
    safe_counts = jnp.maximum(counts, 1.0)
    batch_mean = totals / safe_counts
    batch_square = squares / safe_counts
    updated_return_mean = (1.0 - mixing) * pop_mean + mixing * batch_mean
    mean_gap = batch_mean - pop_mean
    variance = (
        (1.0 - mixing) * pop_scale * pop_scale
        + mixing * (batch_square - batch_mean * batch_mean)
        + mixing * (1.0 - mixing) * mean_gap * mean_gap
    )
    return (updated_return_mean, jnp.sqrt(variance))


def rescale_head(w_head, head_bias, pop_mean, pop_scale, updated_return_mean, updated_return_scale):
    scale_ratio = pop_scale / updated_return_scale
    column_scale = jnp.concatenate([jnp.ones((ACTIONS,), jnp.float32), scale_ratio])
    new_head = (w_head.astype(jnp.float32) * column_scale[None, :]).astype(jnp.bfloat16)
    value_bias = (
        pop_scale * head_bias[ACTIONS:] + pop_mean - updated_return_mean
    ) / updated_return_scale
    new_bias = jnp.concatenate([head_bias[:ACTIONS], value_bias])
    return (new_head, new_bias)


def importance_trace_loss(
    head_value_estimates,
    task_indices,
    actions,
    rewards,
    discount_factors,
    behaviour_log_prob,
    updated_return_mean,
    updated_return_scale,
    loss_weighting,
):
    task_table = task_onehot(task_indices)
    env_mean = jnp.dot(task_table, updated_return_mean, precision=lax.Precision.HIGHEST)[:, None]
    env_scale = jnp.dot(task_table, updated_return_scale, precision=lax.Precision.HIGHEST)[:, None]
    logits = head_value_estimates[:, :-1, :ACTIONS]
    norm_values = jnp.sum(head_value_estimates[:, :, ACTIONS:] * task_table[:, None, :], axis=2)
    values = lax.stop_gradient(norm_values * env_scale + env_mean)
    log_total = jnp.log(jnp.sum(jnp.exp(logits), axis=2))
    chosen = actions[:, :, None] == jnp.arange(ACTIONS, dtype=jnp.int32)[None, None, :]
    log_policy = jnp.sum(jnp.where(chosen, logits, 0.0), axis=2) - log_total
    clipped = jnp.minimum(jnp.exp(lax.stop_gradient(log_policy) - behaviour_log_prob), 1.0)
    deltas = clipped * (rewards + discount_factors * values[:, 1:] - values[:, :-1])
    targets = values[:, :-1] + discounted_sums(deltas, discount_factors * clipped)
    following = jnp.concatenate([targets[:, 1:], values[:, -1:]], axis=1)
    advantage = lax.stop_gradient(
        clipped
        * ((rewards + discount_factors * following - env_mean) / env_scale - norm_values[:, :-1])
    )
    normed_targets = lax.stop_gradient((targets - env_mean) / env_scale)
    policy = jnp.exp(logits - log_total[:, :, None])
    entropy = -jnp.sum(policy * (logits - log_total[:, :, None]), axis=2)
    per_frame = (
        -advantage * log_policy
        + 0.5 * BASELINE_COST * (normed_targets - norm_values[:, :-1]) ** 2
        - ENTROPY_COST * entropy
    )
    return loss_weighting * jnp.sum(per_frame)


def on_device(
    observations,
    gain,
    w_in,
    w_mix,
    w_out,
    w_head,
    head_bias,
    pop_mean,
    pop_scale,
    task_indices,
    actions,
    rewards,
    episode_ends,
    behaviour_log_prob,
):
    env_count, frames, part_width = observations.shape
    groups = lax.axis_size("tp")
    full_width = part_width * groups
    row_count = env_count * frames
    local_rows = row_count // groups
    own_tokens = observations.reshape(row_count, part_width)
    discount_factors = DISCOUNT * (1.0 - episode_ends.astype(jnp.float32))
    counts, totals, squares = popart_partials(task_indices, rewards, discount_factors)
    counts, totals, squares = lax.psum((counts, totals, squares), "task")
    updated_return_mean, updated_return_scale = popart_update(
        counts, totals, squares, pop_mean, pop_scale
    )
    new_head, new_bias = rescale_head(
        w_head, head_bias, pop_mean, pop_scale, updated_return_mean, updated_return_scale
    )
    loss_weighting = float(env_count * lax.axis_size("task")) ** (-0.5)
    tokens, gain_all = (
        lax.all_gather(own_tokens, "tp", axis=1, tiled=True),
        lax.all_gather(gain.astype(jnp.bfloat16), "tp", axis=0, tiled=True).astype(gain.dtype),
    )
    row_offset = lax.axis_index("tp") * local_rows
    token_rows = lax.dynamic_slice_in_dim(tokens, row_offset, local_rows, 0)
    pre_in = jnp.dot(tokens, w_in, preferred_element_type=jnp.float32)
    hidden_in = jax.nn.silu(pre_in).astype(jnp.bfloat16)
    hidden_rows = hidden_in
    mix_sum = lax.psum_scatter(
        jnp.dot(hidden_rows, w_mix, preferred_element_type=jnp.float32).astype(jnp.bfloat16),
        "tp",
        scatter_dimension=0,
        tiled=True,
    ).astype(jnp.float32)
    residual = token_rows.astype(jnp.float32) + mix_sum
    inverse = lax.rsqrt(jnp.mean(residual * residual, axis=1, keepdims=True) + NORM_EPS)
    normed = (residual * inverse * gain_all[None, :]).astype(jnp.bfloat16)
    normed_all = lax.all_gather(normed, "tp", axis=0, tiled=True)
    pre_out = jnp.dot(normed_all, w_out, preferred_element_type=jnp.float32)
    hidden_out = jax.nn.silu(pre_out).astype(jnp.bfloat16)
    head_terms = jnp.dot(hidden_out, new_head, preferred_element_type=jnp.float32)
    head_value_estimates = (
        lax.psum(head_terms.astype(jnp.bfloat16), "tp").astype(jnp.float32) + new_bias[None, :]
    )
    head_value_estimates = head_value_estimates.reshape(env_count, frames, -1)

    def group_loss(network_outputs):
        return importance_trace_loss(
            network_outputs,
            task_indices,
            actions,
            rewards,
            discount_factors,
            behaviour_log_prob,
            updated_return_mean,
            updated_return_scale,
            loss_weighting,
        )

    loss_value, pullback = jax.vjp(group_loss, head_value_estimates)
    (d_heads,) = pullback(jnp.ones((), jnp.float32))
    d_rounded = d_heads.reshape(row_count, -1).astype(jnp.bfloat16)
    grad_head = jnp.dot(hidden_out.T, d_rounded, preferred_element_type=jnp.float32)
    grad_bias = jnp.sum(d_rounded.astype(jnp.float32), axis=0)
    d_hidden_out = jnp.dot(d_rounded, new_head.T, preferred_element_type=jnp.float32)
    d_pre_out = (d_hidden_out * silu_slope(pre_out)).astype(jnp.bfloat16)
    grad_out = jnp.dot(normed_all.T, d_pre_out, preferred_element_type=jnp.float32)
    d_normed = lax.psum_scatter(
        jnp.dot(d_pre_out, w_out.T, preferred_element_type=jnp.float32).astype(jnp.bfloat16),
        "tp",
        scatter_dimension=0,
        tiled=True,
    ).astype(jnp.float32)
    scaled = d_normed * gain_all[None, :]
    inner_sum = jnp.sum(scaled * residual, axis=1, keepdims=True)
    d_residual = (inverse * scaled - residual * inverse**3 * inner_sum / full_width).astype(
        jnp.bfloat16
    )
    grad_gain = lax.psum_scatter(
        jnp.sum(d_normed * residual * inverse, axis=0), "tp", scatter_dimension=0, tiled=True
    )
    arrived = lax.all_gather(d_residual, "tp", axis=0, tiled=True)
    hidden_rows = hidden_in
    grad_part = jnp.dot(hidden_rows.T, arrived, preferred_element_type=jnp.float32)
    d_hidden = jnp.dot(arrived, w_mix.T, preferred_element_type=jnp.float32)
    grad_mix = grad_part
    d_pre_in = (d_hidden * silu_slope(pre_in)).astype(jnp.bfloat16)
    grad_in = jnp.dot(tokens.T, d_pre_in, preferred_element_type=jnp.float32)
    grad_in, grad_mix, grad_out, grad_gain, grad_head, grad_bias = (
        lax.psum(grad_in.astype(jnp.bfloat16), "task").astype(jnp.float32),
        lax.psum(grad_mix.astype(jnp.bfloat16), "task").astype(jnp.float32),
        lax.psum(grad_out.astype(jnp.bfloat16), "task").astype(jnp.float32),
        lax.psum(grad_gain.astype(jnp.bfloat16), "task").astype(jnp.float32),
        lax.psum(grad_head.astype(jnp.bfloat16), "task").astype(jnp.float32),
        lax.psum(grad_bias.astype(jnp.bfloat16), "task").astype(jnp.float32),
    )
    return (
        grad_in,
        grad_mix,
        grad_out,
        grad_gain,
        grad_head,
        grad_bias,
        new_head,
        new_bias,
        updated_return_mean,
        updated_return_scale,
    )


def solution(mesh):
    in_specs = (
        P("task", None, "tp"),
        P("tp"),
        P(None, "tp"),
        P("tp", None),
        P(None, "tp"),
        P("tp", None),
        P(),
        P(),
        P(),
        P("task"),
        P("task", None),
        P("task", None),
        P("task", None),
        P("task", None),
    )
    out_specs = (
        P(None, "tp"),
        P("tp", None),
        P(None, "tp"),
        P("tp"),
        P("tp", None),
        P(),
        P("tp", None),
        P(),
        P(),
        P(),
    )
    return jax.shard_map(
        on_device, mesh=mesh, in_specs=in_specs, out_specs=out_specs, check_vma=False
    )
```

profile of v0, /device:TPU:0, one launch (start us, length us, event | category | flops | bytes accessed | tf_op | source)
XLA Modules:
  0.0 621.8 jit_solution(17500189969074934395)
XLA Ops:
  8.0 51.3 %all-gather.5.cloned.1.call-done = bf16[512,4096]{1,0:T(8,128)(2,1)} async-done(((bf16[512,512]{1,0:T(8,128)(2,1)}), bf16[512,4096]{1,0:T(8,128)(2,1)}) %all-gather.5.cloned.1.call-update) | async-done | bytes 4194320 | tf_op jit(solution)/shard_map/all_gather | solution.py:146
  59.2 5.9 fusion.47
  65.1 4.4 convolution_convert_fusion.4
  70.2 13.0 %all-gather = bf16[8,1,512]{2,1,0:T(2,128)(2,1)S(1)} all-gather(bf16[1,1,512]{2,1,0:T(2,128)(2,1)S(1)} %reshape.77), channel_id=1, replica_groups=mesh['task'=4,'tp'=8] {'tp'}, dimensions={0}, use_global_device_ids=true | all-gather | bytes 9216 | tf_op jit(solution)/shard_map/all_gather | solution.py:147
  83.2 35.3 %reduce-scatter.3.cloned.1.call-done = bf16[64,4096]{1,0:T(8,128)(2,1)} async-done(((bf16[512,4096]{1,0:T(8,128)(2,1)}), bf16[64,4096]{1,0:T(8,128)(2,1)}) %reduce-scatter.3.cloned.1.call-update) | async-done | bytes 524304 | tf_op jit(solution)/shard_map/reduce_scatter | solution.py:154
  120.1 2.2 multiply_convert_fusion.1
  124.1 9.9 %all-reduce.5 = (f32[57]{0:T(128)S(1)}, f32[57]{0:T(128)S(1)}, f32[57]{0:T(128)S(1)}) all-reduce(f32[57]{0:T(128)S(1)} %convolution_bitcast_fusion.3, f32[57]{0:T(128)S(1)} %broadcast_multiply_fusion.1, f32[57]{0:T(128)S(1)} %convolution_bitcast_fusion.2), channel_id=1, replica_groups=mesh['task'=4,'tp'=8] {'task'}, use_global_device_ids=true, to_apply=%region_7.8 | all-reduce | flops 171 | bytes 1368 | tf_op jit(solution)/shard_map/psum | solution.py:137
  134.8 33.0 %all-gather.7.cloned.1.call-done = bf16[512,4096]{1,0:T(8,128)(2,1)} async-done(((bf16[64,4096]{1,0:T(8,128)(2,1)}), bf16[512,4096]{1,0:T(8,128)(2,1)}) %all-gather.7.cloned.1.call-update) | async-done | bytes 4194320 | tf_op jit(solution)/shard_map/all_gather | solution.py:163
  167.8 5.9 multiply_convert_fusion
  175.1 49.2 %all-reduce.11.cloned.1.call-done = bf16[512,75]{0,1:T(8,128)(2,1)} async-done(((bf16[512,75]{0,1:T(8,128)(2,1)}), bf16[512,75]{0,1:T(8,128)(2,1)}) %all-reduce.11.cloned.1.call-update) | async-done | bytes 76816 | tf_op jit(solution)/shard_map/psum | solution.py:168
  230.1 4.4 convolution_convert_fusion.3
  234.5 53.4 %reduce-scatter.5.cloned.1.call-done = bf16[64,4096]{1,0:T(8,128)(2,1)} async-done(((bf16[512,4096]{1,0:T(8,128)(2,1)}), bf16[64,4096]{1,0:T(8,128)(2,1)}) %reduce-scatter.5.cloned.1.call-update) | async-done | bytes 524304 | tf_op jit(solution)/shard_map/reduce_scatter | solution.py:193
  287.9 1.7 fusion.13
  289.6 2.4 fusion.10
  293.1 6.6 %convolution_convert_fusion = bf16[4096,512]{1,0:T(8,128)(2,1)} fusion(bf16[512,4096]{1,0:T(8,128)(2,1)} %all-gather.7.cloned.1.call-done, bf16[512,512]{1,0:T(8,128)(2,1)S(1)} %copy-done.21), kind=kOutput, calls=%fused_computation.6 | convolution fusion | flops 2149580800 | bytes 8912896 | tf_op jit(solution)/shard_map/dot_general | solution.py:192
  299.7 37.8 %all-gather.9.cloned.1.call-done = bf16[512,4096]{1,0:T(8,128)(2,1)} async-done(((bf16[64,4096]{1,0:T(8,128)(2,1)}), bf16[512,4096]{1,0:T(8,128)(2,1)}) %all-gather.9.cloned.1.call-update) | async-done | bytes 4194320 | tf_op jit(solution)/shard_map/all_gather | solution.py:207
  337.5 6.6 %convolution_convert_fusion.1 = bf16[512,4096]{1,0:T(8,128)(2,1)} fusion(bf16[512,4096]{1,0:T(8,128)(2,1)} %all-gather.9.cloned.1.call-done, f32[512,512]{1,0:T(8,128)S(1)} %fusion.47), kind=kOutput, calls=%fused_computation.7 | convolution fusion | flops 2150891520 | bytes 9437184 | tf_op jit(solution)/shard_map/dot_general | solution.py:209
  344.1 11.5 %fusion.4 = bf16[4096,512]{0,1:T(8,128)(2,1)} fusion(bf16[512,4096]{1,0:T(8,128)(2,1)} %all-gather.5.cloned.1.call-done, bf16[512,4096]{1,0:T(8,128)(2,1)} %all-gather.9.cloned.1.call-done, bf16[512,4096]{1,0:T(8,128)(2,1)} %param.21, f32[512,512]{1,0:T(8,128)S(1)} %fusion.47), kind=kOutput, calls=%fused_computation.11 | convolution fusion | flops 4299423744 | bytes 17825792 | tf_op jit(solution)/shard_map/dot_general | solution.py:213
  357.5 27.0 %all-reduce.4 = bf16[4096]{0:T(1024)(128)(2,1)S(1)} all-reduce(f32[4096]{0:T(1024)S(1)} %get-tuple-element.294), channel_id=4, replica_groups=mesh['task'=4,'tp'=8] {'tp'}, use_global_device_ids=true, to_apply=%region_24.25.clone | all-reduce | flops 4096 | bytes 24576
  384.6 10.1 %all-reduce.6 = (bf16[512]{0:T(512)(128)(2,1)S(1)}, bf16[75]{0:T(256)(128)(2,1)S(1)}) all-reduce(bf16[512]{0:T(512)(128)(2,1)S(1)} %dynamic-slice.3, bf16[75]{0:T(256)(128)(2,1)S(1)} %get-tuple-element.330), channel_id=1, replica_groups=mesh['task'=4,'tp'=8] {'task'}, use_global_device_ids=true, to_apply=%region_25.26 | all-reduce | flops 587 | bytes 2348 | tf_op jit(solution)/shard_map/psum | solution.py:218
  395.8 200.0 %all-reduce.13.cloned.1.call-done = (bf16[4096,512]{0,1:T(8,128)(2,1)}, bf16[512,4096]{1,0:T(8,128)(2,1)}, bf16[4096,512]{1,0:T(8,128)(2,1)}, bf16[512,75]{0,1:T(8,128)(2,1)}) async-done(((bf16[4096,512]{0,1:T(8,128)(2,1)}, bf16[512,4096]{1,0:T(8,128)(2,1)}, bf16[4096,512]{1,0:T(8,128)(2,1)}, bf16[512,75]{0,1:T(8,128)(2,1)}), (bf16[4096,512]{0,1:T(8,128)(2,1)}, bf16[512,4096]{1,0:T(8,128)(2,1)}, ...) | async-done | bytes 12659728 | tf_op jit(solution)/shard_map/psum | solution.py:215
  595.8 6.8 %convert_element_type.132 = f32[512,4096]{1,0:T(8,128)} convert(bf16[512,4096]{1,0:T(8,128)(2,1)} %get-tuple-element.327) | non-fusion elementwise | flops 2097152 | bytes 12582912 | tf_op jit(solution)/shard_map/convert_element_type | solution.py:216
  602.6 4.6 convert_element_type.134
  607.2 7.1 %copy.47 = f32[4096,512]{1,0:T(8,128)} copy(bf16[4096,512]{0,1:T(8,128)(2,1)} %get-tuple-element.326) | data formatting | bytes 12582912
  (176 shorter events, 18.4 us)
Async XLA Ops:
  7.2 52.0 %all-gather.5.cloned.1.call-start = ((), (), s32[]{:S(2)}) async-start(), calls=%async_computation.2 | async-start | bytes 4718592 | tf_op jit(solution)/shard_map/all_gather | solution.py:146
  7.9 110.7 %reduce-scatter.3.cloned.1.call-start = ((), (), s32[]{:S(2)}) async-start(), calls=%async_computation.3 | async-start | bytes 4718592 | tf_op jit(solution)/shard_map/reduce_scatter | solution.py:154
  69.5 52.8 %copy-start.6 = (s32[32,15]{0,1:T(8,128)S(1)}, s32[32,15]{0,1:T(8,128)}, u32[]{:S(2)}) copy-start(s32[32,15]{0,1:T(8,128)} %param.30) | copy-start | bytes 5764
  69.6 53.0 %copy-start.5 = (f32[32,15]{0,1:T(8,128)S(1)}, f32[32,15]{0,1:T(8,128)}, u32[]{:S(2)}) copy-start(f32[32,15]{0,1:T(8,128)} %param.29) | copy-start | bytes 5764
  69.6 54.1 %copy-start.13 = (s32[32]{0:T(128)S(1)}, s32[32]{0:T(128)}, u32[]{:S(2)}) copy-start(s32[32]{0:T(128)} %param.27) | copy-start | bytes 388
  69.6 64.4 %copy-start.11 = (f32[57]{0:T(128)S(1)}, f32[57]{0:T(128)}, u32[]{:S(2)}) copy-start(f32[57]{0:T(128)} %param.25) | copy-start | bytes 688
  69.6 64.4 %copy-start.12 = (f32[57]{0:T(128)S(1)}, f32[57]{0:T(128)}, u32[]{:S(2)}) copy-start(f32[57]{0:T(128)} %param.26) | copy-start | bytes 688
  69.6 64.4 %copy-start.14 = (f32[75]{0:T(128)S(1)}, f32[75]{0:T(128)}, u32[]{:S(2)}) copy-start(f32[75]{0:T(128)} %param.24) | copy-start | bytes 904
  69.6 65.0 %copy-start.3 = (bf16[512,75]{0,1:T(8,128)(2,1)S(1)}, bf16[512,75]{0,1:T(8,128)(2,1)}, u32[]{:S(2)}) copy-start(bf16[512,75]{0,1:T(8,128)(2,1)} %param.23) | copy-start | bytes 230404
  69.6 98.2 %all-gather.7.cloned.1.call-start = ((), (), s32[]{:S(2)}) async-start(), calls=%async_computation.4 | async-start | bytes 4718592 | tf_op jit(solution)/shard_map/all_gather | solution.py:163
  122.3 102.0 %all-reduce.11.cloned.1.call-start = ((), (), s32[]{:S(2)}) async-start(), calls=%async_computation.5 | async-start | bytes 163840 | tf_op jit(solution)/shard_map/psum | solution.py:168
  134.0 39.7 %copy-start.15 = (f32[57]{0:T(128)}, f32[57]{0:T(128)S(1)}, u32[]{:S(2)}) copy-start(f32[57]{0:T(128)S(1)} %get-tuple-element.339) | copy-start | bytes 688
  134.0 39.7 %copy-start.16 = (f32[57]{0:T(128)}, f32[57]{0:T(128)S(1)}, u32[]{:S(2)}) copy-start(f32[57]{0:T(128)S(1)} %get-tuple-element.340) | copy-start | bytes 688
  134.7 94.1 %copy-start.2 = (bf16[512,75]{0,1:T(8,128)(2,1)}, bf16[512,75]{0,1:T(8,128)(2,1)S(1)}, u32[]{:S(2)}) copy-start(bf16[512,75]{0,1:T(8,128)(2,1)S(1)} %multiply_convert_fusion.3) | copy-start | bytes 230404
  134.7 40.2 %copy-start.7 = (s32[32,15]{0,1:T(8,128)S(1)}, s32[32,15]{0,1:T(8,128)}, u32[]{:S(2)}) copy-start(s32[32,15]{0,1:T(8,128)} %param.28) | copy-start | bytes 5764
  134.7 40.3 %copy-start.8 = (f32[32,15]{0,1:T(8,128)S(1)}, f32[32,15]{0,1:T(8,128)}, u32[]{:S(2)}) copy-start(f32[32,15]{0,1:T(8,128)} %param.31) | copy-start | bytes 5764
  174.7 113.2 %reduce-scatter.5.cloned.1.call-start = ((), (), s32[]{:S(2)}) async-start(), calls=%async_computation.6 | async-start | bytes 4718592 | tf_op jit(solution)/shard_map/reduce_scatter | solution.py:193
  174.8 54.4 %copy-start.10 = (f32[75]{0:T(128)}, f32[75]{0:T(128)S(1)}, u32[]{:S(2)}) copy-start(f32[75]{0:T(128)S(1)} %pad_maximum_fusion) | copy-start | bytes 904
  234.5 53.5 %copy-start = (bf16[64,4096]{1,0:T(8,128)(2,1)S(1)}, bf16[64,4096]{1,0:T(8,128)(2,1)}, u32[]{:S(2)}) copy-start(bf16[64,4096]{1,0:T(8,128)(2,1)} %reduce-scatter.3.cloned.1.call-done) | copy-start | bytes 1572868
  234.5 58.7 %copy-start.21 = (bf16[512,512]{1,0:T(8,128)(2,1)S(1)}, bf16[512,512]{1,0:T(8,128)(2,1)}, u32[]{:S(2)}) copy-start(bf16[512,512]{1,0:T(8,128)(2,1)} %copy-done.20) | copy-start | bytes 1572868
  234.5 103.0 %all-gather.9.cloned.1.call-start = ((), (), s32[]{:S(2)}) async-start(), calls=%async_computation.7 | async-start | bytes 4718592 | tf_op jit(solution)/shard_map/all_gather | solution.py:207
  292.0 303.8 %all-reduce.13.cloned.1.call-start = ((), (), s32[]{:S(2)}) async-start(), calls=%async_computation.8 | async-start | bytes 25329664 | tf_op jit(solution)/shard_map/psum | solution.py:215
  595.8 6.8 %copy-start.1 = (bf16[4096,512]{1,0:T(8,128)(2,1)S(1)}, bf16[4096,512]{1,0:T(8,128)(2,1)}, u32[]{:S(2)}) copy-start(bf16[4096,512]{1,0:T(8,128)(2,1)} %get-tuple-element.328) | copy-start | bytes 12582916
  607.2 7.1 %copy-start.4 = (bf16[512,75]{0,1:T(8,128)(2,1)S(1)}, bf16[512,75]{0,1:T(8,128)(2,1)}, u32[]{:S(2)}) copy-start(bf16[512,75]{0,1:T(8,128)(2,1)} %get-tuple-element.329) | copy-start | bytes 230404
  (5 other events, 10.2 us)
Sparse Core Ops, SparseCore 0:
  9.6 49.5 all-gather.4
  69.8 48.7 reduce-scatter.2
  122.4 45.3 all-gather.6
  174.8 49.4 all-reduce.10
  234.6 53.2 reduce-scatter.4
  292.1 45.3 all-gather.8
  355.7 239.9 all-reduce.12
where the time goes:
time: 622 us
  waiting for transfers between devices  461 us (74%)
  blocking collectives  60 us (10%)
  matrix products  48.3 us (8%)
  other arithmetic  24.8 us (4%)
  between operations  15.1 us (2%)
  local copies, waits for them, and re-layouts  12 us (2%)
    psum x1, waiting for transfers between devices, on_device(): lax.psum(grad_in.astype(jnp.bfloat16), 'task').astype(jnp.float32)  200 us
    reduce_scatter x1, waiting for transfers between devices, on_device(): lax.psum_scatter(jnp.dot(d_pre_out, w_out.T, preferred_element_type=jnp.f...  53.4 us
    all_gather x1, waiting for transfers between devices, on_device(): lax.all_gather(own_tokens, 'tp', axis=1, tiled=True)  51.3 us
    psum x1, waiting for transfers between devices, on_device(): lax.psum(head_terms.astype(jnp.bfloat16), 'tp').astype(jnp.float32)  49.2 us
    all_gather x1, waiting for transfers between devices, on_device(): arrived = lax.all_gather(d_residual, 'tp', axis=0, tiled=True)  37.8 us
    reduce_scatter x1, waiting for transfers between devices, on_device(): lax.psum_scatter(jnp.dot(hidden_rows, w_mix, preferred_element_type=jnp.f...  35.3 us
    all_gather x1, waiting for transfers between devices, on_device(): normed_all = lax.all_gather(normed, 'tp', axis=0, tiled=True)  33 us
    unnamed x1, blocking collectives  27 us
  transfers between devices with their start and end apart: 7, of which 7 were waited for; matrix products, arithmetic and copies ran while one was open for 2% of the time, Pallas kernels for 0%

commit v1 on v0

--- a/solution.py
+++ b/solution.py
@@ -165,7 +165,8 @@
     hidden_out = jax.nn.silu(pre_out).astype(jnp.bfloat16)
     head_terms = jnp.dot(hidden_out, new_head, preferred_element_type=jnp.float32)
     head_value_estimates = (
-        lax.psum(head_terms.astype(jnp.bfloat16), "tp").astype(jnp.float32) + new_bias[None, :]
+        jnp.sum(lax.all_gather(head_terms.astype(jnp.bfloat16), "tp"), axis=0).astype(jnp.float32)
+        + new_bias[None, :]
     )
     head_value_estimates = head_value_estimates.reshape(env_count, frames, -1)
 

time: 622 us -> 582 us (0.936)
  waiting for transfers between devices: 461 us -> 407 us
  blocking collectives: 60 us -> 75.1 us
    psum x1 -> x0, waiting for transfers between devices: 49.2 us -> none  [on_device(): lax.psum(head_terms.astype(jnp.bfloat16), 'tp').astype(jnp.float32)]
    all_gather x0 -> x1, blocking collectives: none -> 15.2 us  [on_device(): lax.all_gather(head_terms.astype(jnp.bfloat16), 'tp')]
  transfers between devices with their start and end apart: 7 -> 6, of which waited for: 7 -> 6; matrix products, arithmetic and copies ran while one was open for 2% -> 2% of each run, Pallas kernels for 0% -> 0%
where the time goes in v1:
time: 582 us
  waiting for transfers between devices  407 us (70%)
  blocking collectives  75.1 us (13%)
  matrix products  47.6 us (8%)
  other arithmetic  24.2 us (4%)
  between operations  15.1 us (3%)
  local copies, waits for them, and re-layouts  12.2 us (2%)
    psum x1, waiting for transfers between devices, on_device(): lax.psum(grad_in.astype(jnp.bfloat16), 'task').astype(jnp.float32)  200 us
    all_gather x1, waiting for transfers between devices, on_device(): lax.all_gather(own_tokens, 'tp', axis=1, tiled=True)  51.3 us
    reduce_scatter x1, waiting for transfers between devices, on_device(): lax.psum_scatter(jnp.dot(d_pre_out, w_out.T, preferred_element_type=jnp.f...  48.6 us
    all_gather x1, waiting for transfers between devices, on_device(): arrived = lax.all_gather(d_residual, 'tp', axis=0, tiled=True)  38 us
    reduce_scatter x1, waiting for transfers between devices, on_device(): lax.psum_scatter(jnp.dot(hidden_rows, w_mix, preferred_element_type=jnp.f...  35.3 us
    all_gather x1, waiting for transfers between devices, on_device(): normed_all = lax.all_gather(normed, 'tp', axis=0, tiled=True)  32.7 us
    unnamed x1, blocking collectives  27 us
    all_gather x1, blocking collectives, on_device(): lax.all_gather(head_terms.astype(jnp.bfloat16), 'tp')  15.2 us
  transfers between devices with their start and end apart: 6, of which 6 were waited for; matrix products, arithmetic and copies ran while one was open for 2% of the time, Pallas kernels for 0%

profile of v1, /device:TPU:0, one launch (start us, length us, event | category | flops | bytes accessed | tf_op | source)
XLA Modules:
  0.0 581.8 jit_solution(11294245091103800868)
XLA Ops:
  8.0 51.3 %all-gather.6.cloned.1.call-done = bf16[512,4096]{1,0:T(8,128)(2,1)} async-done(((bf16[512,512]{1,0:T(8,128)(2,1)}), bf16[512,4096]{1,0:T(8,128)(2,1)}) %all-gather.6.cloned.1.call-update) | async-done | bytes 4194320 | tf_op jit(solution)/shard_map/all_gather | solution.py:146
  59.2 5.9 %fusion.47 = f32[512,512]{1,0:T(8,128)S(1)} fusion(bf16[512,4096]{1,0:T(8,128)(2,1)} %all-gather.6.cloned.1.call-done, bf16[4096,512]{1,0:T(8,128)(2,1)} %param.20), kind=kOutput, calls=%fused_computation.104 | convolution fusion | flops 2147483648 | bytes 9437184 | tf_op jit(solution)/shard_map/dot_general | solution.py:151
  65.2 4.4 convolution_convert_fusion.4
  70.3 13.0 %all-gather.1 = bf16[8,1,512]{2,1,0:T(2,128)(2,1)S(1)} all-gather(bf16[1,1,512]{2,1,0:T(2,128)(2,1)S(1)} %reshape.84), channel_id=1, replica_groups=mesh['task'=4,'tp'=8] {'tp'}, dimensions={0}, use_global_device_ids=true | all-gather | bytes 9216 | tf_op jit(solution)/shard_map/all_gather | solution.py:147
  83.3 35.3 %reduce-scatter.3.cloned.1.call-done = bf16[64,4096]{1,0:T(8,128)(2,1)} async-done(((bf16[512,4096]{1,0:T(8,128)(2,1)}), bf16[64,4096]{1,0:T(8,128)(2,1)}) %reduce-scatter.3.cloned.1.call-update) | async-done | bytes 524304 | tf_op jit(solution)/shard_map/reduce_scatter | solution.py:154
  120.1 2.2 multiply_convert_fusion.1
  124.2 9.8 %all-reduce.5 = (f32[57]{0:T(128)S(1)}, f32[57]{0:T(128)S(1)}, f32[57]{0:T(128)S(1)}) all-reduce(f32[57]{0:T(128)S(1)} %convolution_bitcast_fusion.3, f32[57]{0:T(128)S(1)} %broadcast_multiply_fusion.1, f32[57]{0:T(128)S(1)} %convolution_bitcast_fusion.2), channel_id=1, replica_groups=mesh['task'=4,'tp'=8] {'task'}, use_global_device_ids=true, to_apply=%region_7.8 | all-reduce | flops 171 | bytes 1368 | tf_op jit(solution)/shard_map/psum | solution.py:137
  135.1 32.7 %all-gather.8.cloned.1.call-done = bf16[512,4096]{1,0:T(8,128)(2,1)} async-done(((bf16[64,4096]{1,0:T(8,128)(2,1)}), bf16[512,4096]{1,0:T(8,128)(2,1)}) %all-gather.8.cloned.1.call-update) | async-done | bytes 4194320 | tf_op jit(solution)/shard_map/all_gather | solution.py:163
  167.8 5.9 %multiply_convert_fusion = (bf16[512,512]{1,0:T(8,128)(2,1)S(1)}, f32[512,512]{1,0:T(8,128)S(1)}) fusion(bf16[512,4096]{1,0:T(8,128)(2,1)} %all-gather.8.cloned.1.call-done, bf16[4096,512]{1,0:T(8,128)(2,1)} %param.22), kind=kOutput, calls=%fused_computation.31 | convolution fusion | flops 2148794368 | bytes 9961472 | tf_op jit(solution)/shard_map/dot_general | solution.py:164
  174.1 15.2 %all-gather = bf16[4096,75]{0,1:T(8,128)(2,1)S(1)} all-gather(bf16[512,75]{0,1:T(8,128)(2,1)S(1)} %convolution_convert_fusion.6), channel_id=2, replica_groups=mesh['task'=4,'tp'=8] {'tp'}, dimensions={0}, use_global_device_ids=true | all-gather | bytes 691200 | tf_op jit(solution)/shard_map/all_gather | solution.py:168
  194.7 4.4 convolution_convert_fusion.3
  199.4 48.6 %reduce-scatter.5.cloned.1.call-done = bf16[64,4096]{1,0:T(8,128)(2,1)} async-done(((bf16[512,4096]{1,0:T(8,128)(2,1)}), bf16[64,4096]{1,0:T(8,128)(2,1)}) %reduce-scatter.5.cloned.1.call-update) | async-done | bytes 524304 | tf_op jit(solution)/shard_map/reduce_scatter | solution.py:194
  248.0 1.7 fusion.13
  249.7 2.4 fusion.10
  253.0 6.6 %convolution_convert_fusion = bf16[4096,512]{1,0:T(8,128)(2,1)} fusion(bf16[512,4096]{1,0:T(8,128)(2,1)} %all-gather.8.cloned.1.call-done, bf16[512,512]{1,0:T(8,128)(2,1)S(1)} %copy-done.21), kind=kOutput, calls=%fused_computation.6 | convolution fusion | flops 2149580800 | bytes 8912896 | tf_op jit(solution)/shard_map/dot_general | solution.py:193
  259.6 38.0 %all-gather.10.cloned.1.call-done = bf16[512,4096]{1,0:T(8,128)(2,1)} async-done(((bf16[64,4096]{1,0:T(8,128)(2,1)}), bf16[512,4096]{1,0:T(8,128)(2,1)}) %all-gather.10.cloned.1.call-update) | async-done | bytes 4194320 | tf_op jit(solution)/shard_map/all_gather | solution.py:208
  297.6 6.6 %convolution_convert_fusion.1 = bf16[512,4096]{1,0:T(8,128)(2,1)} fusion(bf16[512,4096]{1,0:T(8,128)(2,1)} %all-gather.10.cloned.1.call-done, f32[512,512]{1,0:T(8,128)S(1)} %fusion.47), kind=kOutput, calls=%fused_computation.7 | convolution fusion | flops 2150891520 | bytes 9437184 | tf_op jit(solution)/shard_map/dot_general | solution.py:210
  304.2 11.4 %fusion.4 = bf16[4096,512]{0,1:T(8,128)(2,1)} fusion(bf16[512,4096]{1,0:T(8,128)(2,1)} %all-gather.6.cloned.1.call-done, bf16[512,4096]{1,0:T(8,128)(2,1)} %all-gather.10.cloned.1.call-done, bf16[512,4096]{1,0:T(8,128)(2,1)} %param.21, f32[512,512]{1,0:T(8,128)S(1)} %fusion.47), kind=kOutput, calls=%fused_computation.11 | convolution fusion | flops 4299423744 | bytes 17825792 | tf_op jit(solution)/shard_map/dot_general | solution.py:214
  317.5 27.0 %all-reduce.4 = bf16[4096]{0:T(1024)(128)(2,1)S(1)} all-reduce(f32[4096]{0:T(1024)S(1)} %get-tuple-element.304), channel_id=5, replica_groups=mesh['task'=4,'tp'=8] {'tp'}, use_global_device_ids=true, to_apply=%region_24.25.clone | all-reduce | flops 4096 | bytes 24576
  344.6 10.1 %all-reduce.6 = (bf16[512]{0:T(512)(128)(2,1)S(1)}, bf16[75]{0:T(256)(128)(2,1)S(1)}) all-reduce(bf16[512]{0:T(512)(128)(2,1)S(1)} %dynamic-slice.3, bf16[75]{0:T(256)(128)(2,1)S(1)} %get-tuple-element.340), channel_id=1, replica_groups=mesh['task'=4,'tp'=8] {'task'}, use_global_device_ids=true, to_apply=%region_25.26 | all-reduce | flops 587 | bytes 2348 | tf_op jit(solution)/shard_map/psum | solution.py:219
  355.8 200.0 %all-reduce.10.cloned.1.call-done = (bf16[4096,512]{0,1:T(8,128)(2,1)}, bf16[512,4096]{1,0:T(8,128)(2,1)}, bf16[4096,512]{1,0:T(8,128)(2,1)}, bf16[512,75]{0,1:T(8,128)(2,1)}) async-done(((bf16[4096,512]{0,1:T(8,128)(2,1)}, bf16[512,4096]{1,0:T(8,128)(2,1)}, bf16[4096,512]{1,0:T(8,128)(2,1)}, bf16[512,75]{0,1:T(8,128)(2,1)}), (bf16[4096,512]{0,1:T(8,128)(2,1)}, bf16[512,4096]{1,0:T(8,128)(2,1)}, ...) | async-done | bytes 12659728 | tf_op jit(solution)/shard_map/psum | solution.py:216
  555.8 6.8 %convert_element_type.139 = f32[512,4096]{1,0:T(8,128)} convert(bf16[512,4096]{1,0:T(8,128)(2,1)} %get-tuple-element.337) | non-fusion elementwise | flops 2097152 | bytes 12582912 | tf_op jit(solution)/shard_map/convert_element_type | solution.py:217
  562.6 4.6 convert_element_type.141
  567.2 7.1 %copy.53 = f32[4096,512]{1,0:T(8,128)} copy(bf16[4096,512]{0,1:T(8,128)(2,1)} %get-tuple-element.336) | data formatting | bytes 12582912
  (176 shorter events, 17.4 us)
Async XLA Ops:
  7.2 52.0 %all-gather.6.cloned.1.call-start = ((), (), s32[]{:S(2)}) async-start(), calls=%async_computation.2 | async-start | bytes 4718592 | tf_op jit(solution)/shard_map/all_gather | solution.py:146
  7.9 110.7 %reduce-scatter.3.cloned.1.call-start = ((), (), s32[]{:S(2)}) async-start(), calls=%async_computation.3 | async-start | bytes 4718592 | tf_op jit(solution)/shard_map/reduce_scatter | solution.py:154
  59.2 5.9 %copy-start.18 = (bf16[512,4096]{1,0:T(8,128)(2,1)S(1)}, bf16[512,4096]{1,0:T(8,128)(2,1)}, u32[]{:S(2)}) copy-start(bf16[512,4096]{1,0:T(8,128)(2,1)} %param.21) | copy-start | bytes 12582916
  69.6 52.8 %copy-start.6 = (s32[32,15]{0,1:T(8,128)S(1)}, s32[32,15]{0,1:T(8,128)}, u32[]{:S(2)}) copy-start(s32[32,15]{0,1:T(8,128)} %param.30) | copy-start | bytes 5764
  69.6 53.0 %copy-start.5 = (f32[32,15]{0,1:T(8,128)S(1)}, f32[32,15]{0,1:T(8,128)}, u32[]{:S(2)}) copy-start(f32[32,15]{0,1:T(8,128)} %param.29) | copy-start | bytes 5764
  69.6 54.2 %copy-start.14 = (s32[32]{0:T(128)S(1)}, s32[32]{0:T(128)}, u32[]{:S(2)}) copy-start(s32[32]{0:T(128)} %param.27) | copy-start | bytes 388
  69.6 64.5 %copy-start.11 = (f32[57]{0:T(128)S(1)}, f32[57]{0:T(128)}, u32[]{:S(2)}) copy-start(f32[57]{0:T(128)} %param.25) | copy-start | bytes 688
  69.6 64.5 %copy-start.12 = (f32[57]{0:T(128)S(1)}, f32[57]{0:T(128)}, u32[]{:S(2)}) copy-start(f32[57]{0:T(128)} %param.26) | copy-start | bytes 688
  69.6 64.5 %copy-start.13 = (f32[75]{0:T(128)S(1)}, f32[75]{0:T(128)}, u32[]{:S(2)}) copy-start(f32[75]{0:T(128)} %param.24) | copy-start | bytes 904
  69.6 64.6 %copy-start.7 = (s32[32,15]{0,1:T(8,128)S(1)}, s32[32,15]{0,1:T(8,128)}, u32[]{:S(2)}) copy-start(s32[32,15]{0,1:T(8,128)} %param.28) | copy-start | bytes 5764
  69.6 64.6 %copy-start.8 = (f32[32,15]{0,1:T(8,128)S(1)}, f32[32,15]{0,1:T(8,128)}, u32[]{:S(2)}) copy-start(f32[32,15]{0,1:T(8,128)} %param.31) | copy-start | bytes 5764
  69.6 65.3 %copy-start.3 = (bf16[512,75]{0,1:T(8,128)(2,1)S(1)}, bf16[512,75]{0,1:T(8,128)(2,1)}, u32[]{:S(2)}) copy-start(bf16[512,75]{0,1:T(8,128)(2,1)} %param.23) | copy-start | bytes 230404
  69.7 98.2 %all-gather.8.cloned.1.call-start = ((), (), s32[]{:S(2)}) async-start(), calls=%async_computation.4 | async-start | bytes 4718592 | tf_op jit(solution)/shard_map/all_gather | solution.py:163
  122.3 125.7 %reduce-scatter.5.cloned.1.call-start = ((), (), s32[]{:S(2)}) async-start(), calls=%async_computation.5 | async-start | bytes 4718592 | tf_op jit(solution)/shard_map/reduce_scatter | solution.py:194
  134.1 39.6 %copy-start.15 = (f32[57]{0:T(128)}, f32[57]{0:T(128)S(1)}, u32[]{:S(2)}) copy-start(f32[57]{0:T(128)S(1)} %get-tuple-element.349) | copy-start | bytes 688
  134.1 39.7 %copy-start.16 = (f32[57]{0:T(128)}, f32[57]{0:T(128)S(1)}, u32[]{:S(2)}) copy-start(f32[57]{0:T(128)S(1)} %get-tuple-element.350) | copy-start | bytes 688
  134.5 55.5 %copy-start.10 = (f32[75]{0:T(128)}, f32[75]{0:T(128)S(1)}, u32[]{:S(2)}) copy-start(f32[75]{0:T(128)S(1)} %pad_maximum_fusion) | copy-start | bytes 904
  135.1 58.4 %copy-start.2 = (bf16[512,75]{0,1:T(8,128)(2,1)}, bf16[512,75]{0,1:T(8,128)(2,1)S(1)}, u32[]{:S(2)}) copy-start(bf16[512,75]{0,1:T(8,128)(2,1)S(1)} %multiply_convert_fusion.3) | copy-start | bytes 230404
  199.1 48.9 %copy-start = (bf16[64,4096]{1,0:T(8,128)(2,1)S(1)}, bf16[64,4096]{1,0:T(8,128)(2,1)}, u32[]{:S(2)}) copy-start(bf16[64,4096]{1,0:T(8,128)(2,1)} %reduce-scatter.3.cloned.1.call-done) | copy-start | bytes 1572868
  199.1 53.9 %copy-start.21 = (bf16[512,512]{1,0:T(8,128)(2,1)S(1)}, bf16[512,512]{1,0:T(8,128)(2,1)}, u32[]{:S(2)}) copy-start(bf16[512,512]{1,0:T(8,128)(2,1)} %copy-done.20) | copy-start | bytes 1572868
  199.2 98.4 %all-gather.10.cloned.1.call-start = ((), (), s32[]{:S(2)}) async-start(), calls=%async_computation.6 | async-start | bytes 4718592 | tf_op jit(solution)/shard_map/all_gather | solution.py:208
  252.1 303.7 %all-reduce.10.cloned.1.call-start = ((), (), s32[]{:S(2)}) async-start(), calls=%async_computation.7 | async-start | bytes 25329664 | tf_op jit(solution)/shard_map/psum | solution.py:216
  555.8 6.8 %copy-start.1 = (bf16[4096,512]{1,0:T(8,128)(2,1)S(1)}, bf16[4096,512]{1,0:T(8,128)(2,1)}, u32[]{:S(2)}) copy-start(bf16[4096,512]{1,0:T(8,128)(2,1)} %get-tuple-element.338) | copy-start | bytes 12582916
  567.2 7.1 %copy-start.4 = (bf16[512,75]{0,1:T(8,128)(2,1)S(1)}, bf16[512,75]{0,1:T(8,128)(2,1)}, u32[]{:S(2)}) copy-start(bf16[512,75]{0,1:T(8,128)(2,1)} %get-tuple-element.339) | copy-start | bytes 230404
  (4 other events, 4.3 us)
Sparse Core Ops, SparseCore 0:
  9.6 49.5 all-gather.5
  69.8 48.7 reduce-scatter.2
  122.4 45.3 all-gather.7
  199.3 48.6 reduce-scatter.4
  252.2 45.3 all-gather.9
  315.8 239.9 all-reduce.9
